TPU v7x, 256 devices: a whole 4x4x8 slice. The times are simulated.
256 devices in a mesh: dp: 2 (over x_hi), ep: 128 (over x_lo, z, y, core).
Axes of the slice: x: 4 (x_hi: 2, x_lo: 2; x = x_hi * 2 + x_lo), y: 4, z: 8, core: 2. Of those that a mesh axis runs over, the one named last changes fastest.
Arguments:
- tokens: bfloat16 [65536, 512], P(('dp', 'ep')), parts along dimension 0, may hold values from -6 to 6
- routes: int32 [65536, 2], P(('dp', 'ep')), parts along dimension 0, may hold values from 0 to 127, all different within a row; in each aligned block of 256 rows (0 to 255, 256 to 511, ...) at most 8 rows name the same one
- capacity: int32 [128], replicated, may hold values from 4 to 8, as said below
- expert_in: bfloat16 [128, 512, 2048], P('ep'), may hold values from -0.25 to 0.25
- expert_out: bfloat16 [128, 2048, 512], P('ep'), may hold values from -0.125 to 0.125
- shared_in: bfloat16 [2, 2048, 512], P(None, 'ep'), may hold values from -0.25 to 0.25
- shared_out: bfloat16 [2, 2048, 512], P(None, 'ep'), may hold values from -0.125 to 0.125
- route_gate: bfloat16 [128, 6144], P('ep'), may hold values from -0.25 to 0.25
- shared_gate: bfloat16 [2, 6144], replicated, may hold values from -0.25 to 0.25
Outputs:
- mixed: bfloat16 [65536, 12, 512], P(('dp', 'ep')), parts along dimension 0
There are 2 independent parts, one for each index of `dp`. A program takes and returns all parts, laid end to end along the dimension named above; an argument that names none is the same for every part. Nothing has to cross between parts.
Inputs may be any that keep to these rules, and one draw needn't show every extreme that they name: `routes`: each sample names 2 different experts. Within each device's block of 256 samples no expert is named more than 8 times. `capacity`: some expert accepts exactly 8 rows.
All inputs are finite; a program needn't handle non-finite values.
Results may differ from a plain program's by a relative error of at most 0.0054.
Values may be sent and summed in bfloat16 or wider, within the bound.
A program may use at most 64 MiB of HBM per device.

v0:
```python
import jax
import jax.numpy as jnp
from jax import lax
from jax.sharding import Mesh
from jax.sharding import PartitionSpec as P

EP = ("ep_0", "ep_1", "ep_2", "ep_3")
DP_EP = ("dp", "ep_0", "ep_1", "ep_2", "ep_3")


def in_one_piece(arrays, axis, dim, along):
    both = jnp.concatenate(arrays, axis=along)
    whole, at, finished = (lax.all_gather(both, axis, axis=dim, tiled=True), 0, [])
    for a in arrays:
        finished.append(lax.slice_in_dim(whole, at, at + a.shape[along], axis=along))
        at += a.shape[along]
    return tuple(finished)


def split_up(array, dim, devices):
    lengths = array.shape
    parts = array.reshape(*lengths[:dim], devices, lengths[dim] // devices, *lengths[dim + 1 :])
    return jnp.moveaxis(parts, dim, 0)


def laid_out(parts, dim):
    lengths = list(parts.shape[1:])
    lengths[dim] *= parts.shape[0]
    return jnp.moveaxis(parts, 0, dim).reshape(lengths)


def turned_blocks(parts, axes, order):
    lengths = [lax.axis_size(a) for a in axes]
    parts = parts.reshape(*lengths, *parts.shape[1:])
    for k in order:
        parts = lax.all_to_all(parts, axes[k], split_axis=k, concat_axis=k, tiled=True)
    return parts.reshape(-1, *parts.shape[len(axes) :])


def exchange_by_chip(array, groups, order, split_dim, concat_dim):
    devices = lax.axis_size(groups[0]) * lax.axis_size(groups[1])
    parts = split_up(array, split_dim, devices)
    return laid_out(turned_blocks(parts, groups, order), concat_dim)


def exchange_in_groups(array, axis, split_dim, concat_dim, work, item_dim, out_dim):
    items = jax.tree.leaves(array)[0].shape[item_dim]
    count = 2 if items % 2 == 0 else 1
    finished = []
    for k in range(count):
        group = jax.tree.map(
            lambda a: lax.slice_in_dim(
                a, k * (items // count), (k + 1) * (items // count), axis=item_dim
            ),
            array,
        )
        finished.append(
            work(
                lax.all_to_all(
                    group, axis, split_axis=split_dim, concat_axis=concat_dim, tiled=True
                )
            )
        )
    return jax.tree.map(lambda *parts: jnp.concatenate(parts, axis=out_dim), *finished)


def slot_table(routes, capacity, experts, depth):
    pairs = routes.reshape(-1)
    count = pairs.shape[0]
    chosen = pairs[:, None] == jnp.arange(experts, dtype=jnp.int32)[None, :]
    lower = (jnp.arange(count)[:, None] > jnp.arange(count)[None, :]).astype(jnp.bfloat16)
    before = jnp.dot(lower, chosen.astype(jnp.bfloat16), preferred_element_type=jnp.float32)
    ranked = jnp.sum(jnp.where(chosen, before, 0.0), axis=1).astype(jnp.int32)
    limit = jnp.sum(jnp.where(chosen, capacity[None, :], 0), axis=1)
    kept = ranked < limit
    slots = jnp.minimum(pairs * depth + ranked, experts * depth - 1)
    target = jnp.where(kept, slots, experts * depth)
    source = jnp.full((experts * depth,), -1, jnp.int32)
    source = source.at[target].set(
        jnp.arange(count, dtype=jnp.int32) // routes.shape[1], mode="drop"
    )
    return (kept, slots, source)


def on_device(
    tokens, routes, capacity, expert_in, expert_out, shared_in, shared_out, route_gate, shared_gate
):
    experts = lax.axis_size(EP)
    rows_here = tokens.shape[0]
    width = tokens.shape[1]
    top = routes.shape[1]
    shared_count = shared_gate.shape[0]
    tasks = shared_gate.shape[1] // width
    depth = max(4, 4 * rows_here // experts)
    kept, slots, source = slot_table(routes, capacity, experts, depth)
    filled = jnp.where(
        source[:, None] >= 0, tokens[jnp.maximum(source, 0)], jnp.zeros((), jnp.bfloat16)
    )
    outgoing = filled.reshape(experts, depth, width)

    def expert_rows(rows):
        flat = rows.reshape(-1, width)
        hidden = jax.nn.gelu(
            jnp.dot(flat, expert_in[0], preferred_element_type=jnp.float32)
        ).astype(jnp.bfloat16)
        result = jnp.dot(hidden, expert_out[0], preferred_element_type=jnp.float32).astype(
            jnp.bfloat16
        )
        return result.reshape(rows.shape)

    up_rows, down_rows = in_one_piece((shared_in, shared_out), EP, 1, 0)
    hidden = jax.nn.gelu(
        jnp.einsum("td,shd->sth", tokens, up_rows, preferred_element_type=jnp.float32)
    ).astype(jnp.bfloat16)
    shared_rows = jnp.einsum("sth,shd->std", hidden, down_rows, preferred_element_type=jnp.float32)
    shared_logits = lax.dot_general(
        tokens,
        shared_gate.reshape(shared_count * tasks, width),
        (((1,), (1,)), ((), ())),
        preferred_element_type=jnp.float32,
    )
    shared_rows, shared_logits = (
        shared_rows,
        shared_logits.astype(jnp.bfloat16).reshape(rows_here, shared_count, tasks),
    )
    gate_rows = route_gate[0].reshape(tasks, width)

    def serve_scored(rows):
        scores = jnp.einsum(
            "ncd,sd->ncs", rows, gate_rows, preferred_element_type=jnp.float32
        ).astype(jnp.bfloat16)
        return (
            exchange_by_chip(expert_rows(rows), (("ep_0", "ep_1", "ep_2"), "ep_3"), (1, 0), 0, 0),
            exchange_by_chip(scores, (("ep_0", "ep_1", "ep_2"), "ep_3"), (1, 0), 0, 0),
        )

    back, back_scores = exchange_in_groups(outgoing, EP, 0, 0, serve_scored, 1, 1)
    route_logits = (
        back_scores.reshape(-1, tasks)[slots].reshape(rows_here, top, tasks).astype(jnp.float32)
    )
    pair_rows = back.reshape(-1, width)[slots].reshape(rows_here, top, width)
    keep = kept.reshape(rows_here, top).astype(jnp.float32)
    routed_values = keep[:, :, None] * jax.nn.sigmoid(route_logits)
    shared_values = jax.nn.sigmoid(shared_logits.astype(jnp.float32))
    total = jnp.sum(routed_values, axis=1) + jnp.sum(shared_values, axis=1)
    mixed = jnp.zeros((rows_here, tasks, width), jnp.float32)
    for k in range(top):
        mixed = (
            mixed
            + (routed_values[:, k] / total)[:, :, None]
            * pair_rows[:, k].astype(jnp.float32)[:, None, :]
        )
    for s in range(shared_count):
        mixed = mixed + (shared_values[:, s] / total)[:, :, None] * shared_rows[s][:, None, :]
    return mixed.astype(jnp.bfloat16)


def solution(mesh):
    finer = Mesh(
        mesh.devices.reshape(mesh.shape["dp"], 2, 8, 4, 2), ("dp", "ep_0", "ep_1", "ep_2", "ep_3")
    )
    in_specs = (
        P(DP_EP, None),
        P(DP_EP, None),
        P(),
        P(EP, None, None),
        P(EP, None, None),
        P(None, EP, None),
        P(None, EP, None),
        P(EP, None),
        P(),
    )
    out_specs = P(DP_EP, None, None)
    return jax.shard_map(
        on_device, mesh=finer, in_specs=in_specs, out_specs=out_specs, check_vma=False
    )
```

profile of v0, /device:TPU:1, one launch (start us, length us, event | category | flops | bytes accessed | tf_op | source)
XLA Modules:
  0.0 260.3 jit_solution(9069651868593900090)
XLA Ops:
  6.5 1.5 pad_maximum_fusion.1
  8.1 0.8 copy.116
  8.9 0.7 broadcast_multiply_fusion.1
  10.1 0.3 fusion.48
  10.4 0.8 select_reduce_fusion
  11.2 0.6 compare_select_fusion
  11.8 2.4 scatter_custom_fusion
  14.4 4.0 %gather_fusion = bf16[1024,512]{1,0:T(8,128)(2,1)S(1)} fusion(bf16[256,512]{1,0:T(8,128)(2,1)S(1)} %copy-done.1, s32[1024]{0:T(1024)S(1)} %maximum_clamp_fusion), kind=kCustom, calls=%fused_computation | custom fusion | bytes 2101248 | tf_op jit(solution)/shard_map/gather | solution.py:97
  18.4 0.2 bitcast_select_fusion
  18.6 1.3 fusion.81
  19.9 14.9 %all-to-all-start.3 = ((bf16[128,4,512]{2,1,0:T(4,128)(2,1)}), bf16[128,4,512]{2,1,0:T(4,128)(2,1)S(1)}, u32[]{:S(2)}, u32[]{:S(2)}) async-start(bf16[128,4,512]{2,1,0:T(4,128)(2,1)} %get-tuple-element.12), calls=%async_computation.3 | async-start | bytes 1048576 | tf_op jit(solution)/shard_map/all_to_all | solution.py:59
  34.9 20.4 %all-to-all-done.3 = bf16[128,4,512]{2,1,0:T(4,128)(2,1)S(1)} async-done(((bf16[128,4,512]{2,1,0:T(4,128)(2,1)}), bf16[128,4,512]{2,1,0:T(4,128)(2,1)S(1)}, u32[]{:S(2)}, u32[]{:S(2)}) %all-to-all-start.3) | async-done | bytes 524320 | tf_op jit(solution)/shard_map/all_to_all | solution.py:59
  55.3 0.2 convolution_convert_fusion
  55.5 0.2 copy.125
  56.0 3.7 %all_to_all.50 = bf16[2,2,1536]{2,1,0:T(2,128)(2,1)S(1)} all-to-all(bf16[2,2,1536]{2,1,0:T(2,128)(2,1)S(1)} %reshape.213), channel_id=1, replica_groups=mesh['dp'=2,'ep_0'=2,'ep_1'=8,'ep_2'=4,'ep_3'=2] {'ep_3'}, dimensions={0} | all-to-all | bytes 24576 | tf_op jit(solution)/shard_map/all_to_all | solution.py:36
  59.7 7.3 %all-to-all-start = ((bf16[128,4,512]{2,1,0:T(4,128)(2,1)}), bf16[128,4,512]{2,1,0:T(4,128)(2,1)S(1)}, u32[]{:S(2)}, u32[]{:S(2)}) async-start(bf16[128,4,512]{2,1,0:T(4,128)(2,1)} %get-tuple-element.11), calls=%async_computation | async-start | bytes 1048576 | tf_op jit(solution)/shard_map/all_to_all | solution.py:59
  67.1 0.8 copy.127
  67.9 19.6 %all-to-all-done = bf16[128,4,512]{2,1,0:T(4,128)(2,1)S(1)} async-done(((bf16[128,4,512]{2,1,0:T(4,128)(2,1)}), bf16[128,4,512]{2,1,0:T(4,128)(2,1)S(1)}, u32[]{:S(2)}, u32[]{:S(2)}) %all-to-all-start) | async-done | bytes 524320 | tf_op jit(solution)/shard_map/all_to_all | solution.py:59
  87.6 0.9 convolution_convert_fusion.1
  88.4 0.9 copy.120
  89.3 0.8 copy.121
  90.0 1.4 reshape.215
  91.5 3.5 %all-to-all-start.1 = ((bf16[2,2,1536]{2,1,0:T(2,128)(2,1)}), bf16[2,2,1536]{2,1,0:T(2,128)(2,1)S(1)}, u32[]{:S(2)}, u32[]{:S(2)}) async-start(bf16[2,2,1536]{2,1,0:T(2,128)(2,1)} %reshape.215), calls=%async_computation.1 | async-start | bytes 24576 | tf_op jit(solution)/shard_map/all_to_all | solution.py:36
  95.0 0.9 reshape.164
  95.9 4.4 %fusion.41 = bf16[512,512]{1,0:T(8,128)(2,1)S(1)} fusion(bf16[1,2048,512]{2,1,0:T(8,128)(2,1)S(1)} %copy-done, bf16[512,512]{1,0:T(8,128)(2,1)} %reshape.164, bf16[1,512,2048]{2,1,0:T(8,128)(2,1)} %param.12), kind=kOutput, calls=%fused_computation.43 | convolution fusion | flops 2157182976 | bytes 5242880 | tf_op jit(solution)/shard_map/dot_general | solution.py:106
  100.3 0.9 reshape_reshape_reshape.7
  101.3 1.2 copy.135
  102.5 0.9 reshape.163
  103.4 5.2 %fusion.38 = bf16[512,512]{1,0:T(8,128)(2,1)} fusion(bf16[1,2048,512]{2,1,0:T(8,128)(2,1)S(1)} %copy-done, bf16[512,512]{1,0:T(8,128)(2,1)} %reshape.163, bf16[1,512,2048]{2,1,0:T(8,128)(2,1)} %param.12), kind=kOutput, calls=%fused_computation.42 | convolution fusion | flops 2157182976 | bytes 5242880 | tf_op jit(solution)/shard_map/dot_general | solution.py:106
  108.6 1.2 reshape_reshape_reshape.6
  109.8 1.0 copy.133
  110.8 4.0 %all_to_all.51 = bf16[64,2,1,4,512]{4,3,0,2,1:T(4,128)(2,1)S(1)} all-to-all(bf16[64,2,1,4,512]{4,3,0,2,1:T(4,128)(2,1)S(1)} %copy.135), channel_id=1, replica_groups=mesh['dp'=2,'ep_0'=2,'ep_1'=8,'ep_2'=4,'ep_3'=2] {'ep_3'}, dimensions={1} | all-to-all | bytes 1048576 | tf_op jit(solution)/shard_map/all_to_all | solution.py:36
  114.8 5.2 %all_to_all.52 = bf16[64,2,1,4,512]{4,3,0,2,1:T(4,128)(2,1)S(1)} all-to-all(bf16[64,2,1,4,512]{4,3,0,2,1:T(4,128)(2,1)} %copy.133), channel_id=1, replica_groups=mesh['dp'=2,'ep_0'=2,'ep_1'=8,'ep_2'=4,'ep_3'=2] {'ep_3'}, dimensions={1} | all-to-all | bytes 1048576 | tf_op jit(solution)/shard_map/all_to_all | solution.py:36
  120.0 6.1 %all-to-all-start.5 = ((bf16[64,2,1,4,12]{4,1,3,2,0:T(2,128)(2,1)}), bf16[64,2,1,4,12]{4,1,3,2,0:T(2,128)(2,1)S(1)}, u32[]{:S(2)}, u32[]{:S(2)}) async-start(bf16[64,2,1,4,12]{4,1,3,2,0:T(2,128)(2,1)} %copy.127), calls=%async_computation.5 | async-start | bytes 262144 | tf_op jit(solution)/shard_map/all_to_all | solution.py:36
  126.1 0.7 reshape.216
  126.8 1.5 copy.122
  128.4 7.7 %all-to-all-done.5 = bf16[64,2,1,4,12]{4,1,3,2,0:T(2,128)(2,1)S(1)} async-done(((bf16[64,2,1,4,12]{4,1,3,2,0:T(2,128)(2,1)}), bf16[64,2,1,4,12]{4,1,3,2,0:T(2,128)(2,1)S(1)}, u32[]{:S(2)}, u32[]{:S(2)}) %all-to-all-start.5) | async-done | bytes 12320 | tf_op jit(solution)/shard_map/all_to_all | solution.py:36
  136.0 5.9 %all-to-all-start.2 = ((bf16[64,2,1,4,12]{4,1,3,2,0:T(2,128)(2,1)}), bf16[64,2,1,4,12]{4,1,3,2,0:T(2,128)(2,1)}, u32[]{:S(2)}, u32[]{:S(2)}) async-start(bf16[64,2,1,4,12]{4,1,3,2,0:T(2,128)(2,1)} %copy.122), calls=%async_computation.2 | async-start | bytes 262144 | tf_op jit(solution)/shard_map/all_to_all | solution.py:36
  142.0 1.0 copy.136
  142.9 8.8 %all-to-all-done.2 = bf16[64,2,1,4,12]{4,1,3,2,0:T(2,128)(2,1)} async-done(((bf16[64,2,1,4,12]{4,1,3,2,0:T(2,128)(2,1)}), bf16[64,2,1,4,12]{4,1,3,2,0:T(2,128)(2,1)}, u32[]{:S(2)}, u32[]{:S(2)}) %all-to-all-start.2) | async-done | bytes 12320 | tf_op jit(solution)/shard_map/all_to_all | solution.py:36
  151.8 4.6 %all-to-all-start.9 = ((bf16[64,2,1,4,512]{4,3,1,2,0:T(4,128)(2,1)}), bf16[64,2,1,4,512]{4,3,1,2,0:T(4,128)(2,1)S(1)}, u32[]{:S(2)}, u32[]{:S(2)}) async-start(bf16[64,2,1,4,512]{4,3,1,2,0:T(4,128)(2,1)} %copy.136), calls=%async_computation.9 | async-start | bytes 1048576 | tf_op jit(solution)/shard_map/all_to_all | solution.py:36
  156.4 1.4 reshape.162
  157.8 0.7 compare_convert_fusion
  158.5 1.5 fusion.53
  160.0 1.0 copy.134
  161.0 9.8 %all-to-all-done.9 = bf16[64,2,1,4,512]{4,3,1,2,0:T(4,128)(2,1)S(1)} async-done(((bf16[64,2,1,4,512]{4,3,1,2,0:T(4,128)(2,1)}), bf16[64,2,1,4,512]{4,3,1,2,0:T(4,128)(2,1)S(1)}, u32[]{:S(2)}, u32[]{:S(2)}) %all-to-all-start.9) | async-done | bytes 524320 | tf_op jit(solution)/shard_map/all_to_all | solution.py:36
  170.8 10.9 %all-to-all-start.7 = ((bf16[64,2,1,4,512]{4,3,1,2,0:T(4,128)(2,1)}), bf16[64,2,1,4,512]{4,3,1,2,0:T(4,128)(2,1)}, u32[]{:S(2)}, u32[]{:S(2)}) async-start(bf16[64,2,1,4,512]{4,3,1,2,0:T(4,128)(2,1)} %copy.134), calls=%async_computation.7 | async-start | bytes 1048576 | tf_op jit(solution)/shard_map/all_to_all | solution.py:36
  181.7 1.3 pad_clamp_fusion
  183.1 0.7 copy.117
  183.7 0.7 reshape.171
  184.6 1.0 copy.123
  185.7 0.2 copy.148
  185.9 1.5 gather_fusion.1
  187.8 0.7 fusion.80
  188.5 0.7 fusion.60
  189.2 6.4 %all-to-all-done.7 = bf16[64,2,1,4,512]{4,3,1,2,0:T(4,128)(2,1)} async-done(((bf16[64,2,1,4,512]{4,3,1,2,0:T(4,128)(2,1)}), bf16[64,2,1,4,512]{4,3,1,2,0:T(4,128)(2,1)}, u32[]{:S(2)}, u32[]{:S(2)}) %all-to-all-start.7) | async-done | bytes 524320 | tf_op jit(solution)/shard_map/all_to_all | solution.py:36
  195.6 1.7 maximum_bitcast_fusion
  197.3 2.6 %gather_fusion.2 = bf16[512,512]{1,0:T(8,128)(2,1)} fusion(bf16[1024,512]{1,0:T(8,128)(2,1)S(1)} %maximum_bitcast_fusion, s32[1024]{0:T(1024)S(1)} %copy-done.5), kind=kCustom, calls=%fused_computation.2 | custom fusion | bytes 1050624 | tf_op jit(solution)/shard_map/gather | solution.py:141
  200.0 1.2 reshape.166
  201.2 0.7 slice_convert_fusion.1
  202.0 38.3 %all-gather.2.cloned.1.call-done = bf16[4,2048,512]{2,1,0:T(8,128)(2,1)} async-done(((bf16[4,16,512]{2,1,0:T(8,128)(2,1)}), bf16[4,2048,512]{2,1,0:T(8,128)(2,1)}) %all-gather.2.cloned.1.call-update) | async-done | bytes 8388624 | tf_op jit(solution)/shard_map/all_gather | solution.py:13
  240.3 8.6 %fusion.24 = f32[2,256,512]{2,1,0:T(8,128)} fusion(bf16[4,2048,512]{2,1,0:T(8,128)(2,1)} %all-gather.2.cloned.1.call-done, bf16[256,512]{1,0:T(8,128)(2,1)S(1)} %copy-done.1), kind=kOutput, calls=%fused_computation.32 | convolution fusion | flops 2156920832 | bytes 13893632 | tf_op jit(solution)/shard_map/sth,shd->std/dot_general | solution.py:115
  248.9 1.3 slice_bitcast_fusion.1
  250.2 3.3 %add_convert_fusion = bf16[256,12,512]{2,0,1:T(8,128)(2,1)} fusion(f32[256,512]{1,0:T(8,128)S(1)} %get-tuple-element.10, f32[256,12]{0,1:T(8,128)S(1)} %get-tuple-element.16, f32[256,512]{1,0:T(8,128)S(1)} %get-tuple-element.9, f32[256,12]{0,1:T(8,128)S(1)} %get-tuple-element.15, f32[256,512]{1,0:T(8,128)S(1)} %get-tuple-element.20, ...), kind=kLoop, calls=%fused_computation.4 | loop fusion | flops 12582912 | bytes 5292032 | tf_op jit(solution)/shard_map/convert_element_type | solution.py:155
  (40 shorter events, 1.8 us)
Async XLA Ops:
  6.5 89.4 %copy-start = (bf16[1,2048,512]{2,1,0:T(8,128)(2,1)S(1)}, bf16[1,2048,512]{2,1,0:T(8,128)(2,1)}, u32[]{:S(2)}) copy-start(bf16[1,2048,512]{2,1,0:T(8,128)(2,1)} %param.13) | copy-start | bytes 6291460
  6.5 7.8 %copy-start.1 = (bf16[256,512]{1,0:T(8,128)(2,1)S(1)}, bf16[256,512]{1,0:T(8,128)(2,1)}, u32[]{:S(2)}) copy-start(bf16[256,512]{1,0:T(8,128)(2,1)} %param.9) | copy-start | bytes 786436
  6.5 233.8 %all-gather.2.cloned.1.call-start = ((), (), s32[]{:S(2)}) async-start(), calls=%async_computation.10 | async-start | bytes 8454144 | tf_op jit(solution)/shard_map/all_gather | solution.py:13
  10.4 4.0 %copy-start.6 = (f32[512]{0:T(512)}, f32[512]{0:T(512)S(1)}, u32[]{:S(2)}) copy-start(f32[512]{0:T(512)S(1)} %fusion.48) | copy-start | bytes 6148
  18.3 16.4 %copy-start.4 = (bf16[1,6144]{1,0:T(2,128)(2,1)S(1)}, bf16[1,6144]{1,0:T(2,128)(2,1)}, u32[]{:S(2)}) copy-start(bf16[1,6144]{1,0:T(2,128)(2,1)} %param.16) | copy-start | bytes 36868
  19.9 35.4 %all-to-all-start.3 = ((bf16[128,4,512]{2,1,0:T(4,128)(2,1)}), bf16[128,4,512]{2,1,0:T(4,128)(2,1)S(1)}, u32[]{:S(2)}, u32[]{:S(2)}) async-start(bf16[128,4,512]{2,1,0:T(4,128)(2,1)} %get-tuple-element.12), calls=%async_computation.3 | async-start | bytes 1048576 | tf_op jit(solution)/shard_map/all_to_all | solution.py:59
  59.7 27.9 %all-to-all-start = ((bf16[128,4,512]{2,1,0:T(4,128)(2,1)}), bf16[128,4,512]{2,1,0:T(4,128)(2,1)S(1)}, u32[]{:S(2)}, u32[]{:S(2)}) async-start(bf16[128,4,512]{2,1,0:T(4,128)(2,1)} %get-tuple-element.11), calls=%async_computation | async-start | bytes 1048576 | tf_op jit(solution)/shard_map/all_to_all | solution.py:59
  91.5 19.3 %all-to-all-start.1 = ((bf16[2,2,1536]{2,1,0:T(2,128)(2,1)}), bf16[2,2,1536]{2,1,0:T(2,128)(2,1)S(1)}, u32[]{:S(2)}, u32[]{:S(2)}) async-start(bf16[2,2,1536]{2,1,0:T(2,128)(2,1)} %reshape.215), calls=%async_computation.1 | async-start | bytes 24576 | tf_op jit(solution)/shard_map/all_to_all | solution.py:36
  120.0 16.0 %all-to-all-start.5 = ((bf16[64,2,1,4,12]{4,1,3,2,0:T(2,128)(2,1)}), bf16[64,2,1,4,12]{4,1,3,2,0:T(2,128)(2,1)S(1)}, u32[]{:S(2)}, u32[]{:S(2)}) async-start(bf16[64,2,1,4,12]{4,1,3,2,0:T(2,128)(2,1)} %copy.127), calls=%async_computation.5 | async-start | bytes 262144 | tf_op jit(solution)/shard_map/all_to_all | solution.py:36
  136.0 15.7 %all-to-all-start.2 = ((bf16[64,2,1,4,12]{4,1,3,2,0:T(2,128)(2,1)}), bf16[64,2,1,4,12]{4,1,3,2,0:T(2,128)(2,1)}, u32[]{:S(2)}, u32[]{:S(2)}) async-start(bf16[64,2,1,4,12]{4,1,3,2,0:T(2,128)(2,1)} %copy.122), calls=%async_computation.2 | async-start | bytes 262144 | tf_op jit(solution)/shard_map/all_to_all | solution.py:36
  151.8 19.0 %all-to-all-start.9 = ((bf16[64,2,1,4,512]{4,3,1,2,0:T(4,128)(2,1)}), bf16[64,2,1,4,512]{4,3,1,2,0:T(4,128)(2,1)S(1)}, u32[]{:S(2)}, u32[]{:S(2)}) async-start(bf16[64,2,1,4,512]{4,3,1,2,0:T(4,128)(2,1)} %copy.136), calls=%async_computation.9 | async-start | bytes 1048576 | tf_op jit(solution)/shard_map/all_to_all | solution.py:36
  170.8 24.9 %copy-start.2 = (bf16[64,2,1,4,512]{4,3,1,2,0:T(4,128)(2,1)}, bf16[64,2,1,4,512]{4,3,1,2,0:T(4,128)(2,1)S(1)}, u32[]{:S(2)}) copy-start(bf16[64,2,1,4,512]{4,3,1,2,0:T(4,128)(2,1)S(1)} %all-to-all-done.9) | copy-start | bytes 1572868
  170.8 24.8 %all-to-all-start.7 = ((bf16[64,2,1,4,512]{4,3,1,2,0:T(4,128)(2,1)}), bf16[64,2,1,4,512]{4,3,1,2,0:T(4,128)(2,1)}, u32[]{:S(2)}, u32[]{:S(2)}) async-start(bf16[64,2,1,4,512]{4,3,1,2,0:T(4,128)(2,1)} %copy.134), calls=%async_computation.7 | async-start | bytes 1048576 | tf_op jit(solution)/shard_map/all_to_all | solution.py:36
  184.5 1.1 copy-start.3
  184.6 12.7 %copy-start.5 = (s32[1024]{0:T(1024)S(1)}, s32[1024]{0:T(1024)}, u32[]{:S(2)}) copy-start(s32[1024]{0:T(1024)} %pad_clamp_fusion) | copy-start | bytes 12292
Sparse Core Ops, SparseCore 0:
  9.2 231.0 all-gather.1
where the time goes:
time: 265 us; the launch traced here: 260 us
  waiting for transfers between devices  111 us (42%)
  starting transfers between devices  53.3 us (20%)
  local copies, waits for them, and re-layouts  35 us (13%)
  matrix products  21.2 us (8%)
  between operations  13.7 us (5%)
  other arithmetic  13.1 us (5%)
  blocking collectives  12.9 us (5%)
    all_to_all x2, waiting for transfers between devices, exchange_in_groups(): lax.all_to_all(group, axis, split_axis=split_dim, concat_axis=concat_dim,...  40 us
    all_gather x1, waiting for transfers between devices, in_one_piece(): lax.all_gather(both, axis, axis=dim, tiled=True)  38.3 us
    all_to_all x5, waiting for transfers between devices, turned_blocks(): lax.all_to_all(parts, axes[k], split_axis=k, concat_axis=k, tiled=True)  32.7 us
    all_to_all x5, starting transfers between devices, turned_blocks(): lax.all_to_all(parts, axes[k], split_axis=k, concat_axis=k, tiled=True)  31.1 us
    all_to_all x2, starting transfers between devices, exchange_in_groups(): lax.all_to_all(group, axis, split_axis=split_dim, concat_axis=concat_dim,...  22.2 us
    all_to_all x3, blocking collectives, turned_blocks(): lax.all_to_all(parts, axes[k], split_axis=k, concat_axis=k, tiled=True)  12.9 us
    dot_general x2, matrix products, expert_rows(): jnp.dot(hidden, expert_out[0], preferred_element_type=jnp.float32)  9.64 us
    dot_general x1, matrix products, on_device(): jnp.einsum('sth,shd->std', hidden, down_rows, preferred_element_type=jnp....  8.59 us
  transfers between devices with their start and end apart: 8, of which 7 were waited for; matrix products, arithmetic and copies ran while one was open for 21% of the time, Pallas kernels for 0%

commit v1 on v0

v1 whole, which is shorter than its diff:
```python
import jax
import jax.numpy as jnp
from jax import lax
from jax.experimental import pallas as pl
from jax.experimental.pallas import tpu as pltpu
from jax.sharding import PartitionSpec as P

BF = jnp.bfloat16
F32 = jnp.float32
I32 = jnp.int32
MESH = pl.DeviceIdType.MESH
D = 512
H = 2048
TASKS = 12
TOK = 256
NEP = 128
CH = 4
PER = NEP // CH


def zstep(i):
    return jnp.where(i % 2 == 1, (i + 1) // 2, (8 - i // 2) % 8)


def split_index(me):
    return me // 64, (me // 8) % 8, (me // 2) % 4, me % 2


def join_index(x, z, y, c):
    return ((x * 8 + z) * 4 + y) * 2 + c


def offset_of(n):
    q, r = n // PER, n % PER
    return q % 2, zstep(r % 8), r // 8, q // 2


def ahead(me, n):
    x, z, y, c = split_index(me)
    dx, dz, dy, dc = offset_of(n)
    return join_index(lax.rem(x + dx, 2), lax.rem(z + dz, 8), lax.rem(y + dy, 4), lax.rem(c + dc, 2))


def behind(me, n):
    x, z, y, c = split_index(me)
    dx, dz, dy, dc = offset_of(n)
    return join_index(lax.rem(x + dx, 2), lax.rem(z + 8 - dz, 8), lax.rem(y + 4 - dy, 4), lax.rem(c + dc, 2))


def gelu(x):
    return jax.nn.gelu(x, approximate=True)


def dot(a, b, dims=((1,), (0,))):
    return lax.dot_general(a, b, (dims, ((), ())), preferred_element_type=F32)


def flat_rows(blocks):
    return blocks.astype(F32).reshape(-1, D).astype(BF)


def block_rows(rows):
    return rows.reshape(-1, 8, D).astype(BF)


def gate_tile(rows, group):
    sub = lax.broadcasted_iota(I32, (16, D), 0)
    tiles = []
    for row in rows:
        tile = jnp.zeros((16, D), F32)
        for s in range(TASKS):
            tile = jnp.where(sub == s, row[:, s * D : (s + 1) * D], tile)
        tiles.append(tile)
    zero = jnp.zeros((16, D), F32)
    picked = [zero if group(g) is None else tiles[group(g)] for g in range(8)]
    return jnp.concatenate(picked, axis=0).astype(BF)


def exchange(
    tok_h, routes_h, cap_h, ein_h, eout_h, sin_h, sout_h, rg_h, sg_h,
    rows_o, w_o,
    routes_v, cap_v, rg_v, sg_v, ein_v, eout_v, xs, wbuf, tokq,
    snd, recv, ret, back, lret, lback, sacc, precv, xsend, xrecv, pacc, slog,
    load_sem, big_sem, dsend, drecv, rsend, rrecv, lsend, lrecv,
    tsend, trecv, xssem, xrsem, zsend, zrecv, ysend, yrecv, psend, precv_sem, osend, orecv,
):
    me = lax.axis_index("ep")
    x, z, y, c = split_index(me)

    barrier = pltpu.get_barrier_semaphore()

    @pl.loop(1, NEP)
    def _(i):
        pl.semaphore_signal(barrier, inc=1, device_id={"ep": lax.rem(me + i, NEP)}, device_id_type=MESH)

    def load(src, dst, k):
        return pltpu.make_async_copy(src, dst, load_sem.at[k])

    loads = [
        load(routes_h, routes_v, 0),
        load(cap_h, cap_v, 1),
        load(tok_h, tokq.at[0], 2),
        load(rg_h, rg_v, 3),
        load(sg_h, sg_v, 4),
        load(sin_h.at[x], wbuf.at[0, 0, 0, 0], 5),
        load(sout_h.at[x], wbuf.at[0, 0, 1, 0], 6),
        load(sin_h.at[1 - x], xs.at[0], 7),
        load(sout_h.at[1 - x], xs.at[1], 8),
    ]
    for k in loads:
        k.start()
    big = [
        pltpu.make_async_copy(ein_h.at[0], ein_v, big_sem.at[0]),
        pltpu.make_async_copy(eout_h.at[0], eout_v, big_sem.at[1]),
    ]
    for k in big:
        k.start()
    for k in loads:
        k.wait()

    expert = lax.broadcasted_iota(I32, (NEP, 1), 0)
    ex, ez, ey, ec = expert // 64, (expert // 8) % 8, (expert // 2) % 4, expert % 2
    dz = (ez - z + 8) % 8
    zi = jnp.where(dz == 0, 0, jnp.where(dz <= 4, 2 * dz - 1, 2 * (8 - dz)))
    place = ((((ec - c + 2) % 2) * 2 + (ex - x + 2) % 2) * 4 + (ey - y + 4) % 4) * 8 + zi
    base = (place * 8).astype(F32)
    named = lax.broadcasted_iota(I32, (NEP, TOK), 0)
    chosen = [(named == routes_v[k : k + 1, :]).astype(F32) for k in range(2)]
    earlier = (
        lax.broadcasted_iota(I32, (TOK, TOK), 0) < lax.broadcasted_iota(I32, (TOK, TOK), 1)
    ).astype(BF)
    before = dot((chosen[0] + chosen[1]).astype(BF), earlier)
    cap = jnp.broadcast_to(cap_v[...].astype(F32), (8, NEP)).astype(BF)
    slots = []
    for k in range(2):
        rank = jnp.sum(chosen[k] * before, axis=0, keepdims=True)
        start = jnp.sum(chosen[k] * base, axis=0, keepdims=True)
        limit = dot(cap, chosen[k].astype(BF))[0:1]
        slots.append(jnp.where(rank < limit, start + rank, -1.0))
    slot_row = [s.astype(I32) for s in slots]
    slot_col = [
        jnp.transpose(jnp.broadcast_to(s, (128, TOK)))[:, 0:1].astype(I32) for s in slots
    ]

    own = tokq[0]
    for q in range(CH):
        at = lax.broadcasted_iota(I32, (TOK, TOK), 0) + q * TOK
        pick = jnp.logical_or(at == slot_row[0], at == slot_row[1]).astype(F32).astype(BF)
        rows = block_rows(dot(pick, own))
        snd[pl.ds(q * PER, PER)] = rows
        if q == 0:
            recv[0:1] = rows[0:1]

    gates = gate_tile([rg_v[...].astype(F32)], lambda g: 0)
    sg = sg_v[...].astype(F32)
    sg_own = jnp.where(x == 0, sg[0:1], sg[1:2])
    sg_other = jnp.where(x == 0, sg[1:2], sg[0:1])
    shared_gates = gate_tile([sg_own, sg_other], lambda g: g % 4 - 2 if g % 4 >= 2 else None)
    slog[...] = dot(own, shared_gates, ((1,), (1,))).astype(BF).astype(F32)

    pl.semaphore_wait(barrier, NEP - 1)

    def remote(src, dst, ss, rs, to):
        return pltpu.make_async_remote_copy(
            src_ref=src, dst_ref=dst, send_sem=ss, recv_sem=rs, device_id={"ep": to}, device_id_type=MESH
        )

    def bytes_of(a, sem):
        return pltpu.make_async_copy(a, a, sem)

    across = join_index(1 - x, z, y, c)
    partner = join_index(x, z, y, 1 - c)
    both = join_index(1 - x, z, y, 1 - c)

    for k in range(2):
        remote(xs.at[k], wbuf.at[0, 0, k, 1], xssem.at[k], xrsem.at[k], across).start()

    def dispatch(q):
        @pl.loop(1 if q == 0 else 0, PER)
        def _(r):
            n = q * PER + r
            remote(snd.at[n], recv.at[n], dsend, drecv.at[q], ahead(me, n)).start()

    dispatch(0)
    for p, to in ((1, partner), (2, across), (3, both)):
        remote(tokq.at[0], tokq.at[p], tsend.at[p], trecv.at[p], to).start()
    for k in range(2):
        remote(xs.at[k], wbuf.at[0, 0, k, 1], xssem.at[k], xrsem.at[k], across).wait()

    @pl.loop(1, 8)
    def _(i):
        to = join_index(x, lax.rem(z + zstep(i), 8), y, c)
        remote(wbuf.at[0, 0], wbuf.at[0, i], zsend, zrecv, to).start()

    for q in range(1, CH):
        dispatch(q)
    for k in big:
        k.wait()

    fold = (
        lax.broadcasted_iota(I32, (TOK, 128), 1) // 16 == lax.broadcasted_iota(I32, (TOK, 128), 0) % 8
    )

    def serve(q):
        first = 1 if q == 0 else 0
        got = recv.at[pl.ds(q * PER + first, PER - first)]
        bytes_of(got, drecv.at[q]).wait()
        rows = flat_rows(recv[pl.ds(q * PER, PER)])
        total = jnp.zeros((TOK, D), F32)
        for t in range(4):
            hidden = gelu(dot(rows, ein_v[:, t * 512 : (t + 1) * 512])).astype(BF)
            total = total + dot(hidden, eout_v[t * 512 : (t + 1) * 512, :])
        made = block_rows(total)
        ret[pl.ds(q * PER, PER)] = made
        scores = dot(rows, gates, ((1,), (1,))).astype(BF).astype(F32)
        scores = jnp.sum(
            jnp.where(fold, scores, 0.0).reshape(PER, 8, 128), axis=1, keepdims=True
        )
        lret[pl.ds(q * PER, PER)] = scores
        if q == 0:
            back[0:1] = made[0:1]
            lback[0:1] = scores[0:1]

        @pl.loop(first, PER)
        def _(r):
            n = q * PER + r
            to = behind(me, n)
            remote(ret.at[n], back.at[n], rsend, rrecv.at[q], to).start()
            remote(lret.at[n], lback.at[n], lsend, lrecv, to).start()

    def shared_piece(p):
        up = wbuf[p, :, 0].reshape(256, D)
        down = wbuf[p, :, 1].reshape(256, D)

        @pl.loop(0, 4)
        def _(b):
            hidden = gelu(dot(tokq[b], up, ((1,), (1,)))).astype(BF)
            part = dot(hidden, down)
            if p == 0:
                sacc[b] = part
            else:
                sacc[b] = sacc[b] + part

    serve(0)
    bytes_of(wbuf.at[0, pl.ds(1, 7)], zrecv).wait()
    for dy in (1, 3, 2):
        to = join_index(x, z, lax.rem(y + dy, 4), c)
        remote(wbuf.at[0], wbuf.at[dy], ysend.at[dy], yrecv.at[dy], to).start()
    for p, to in ((1, partner), (2, across), (3, both)):
        remote(tokq.at[0], tokq.at[p], tsend.at[p], trecv.at[p], to).wait()
    shared_piece(0)
    for q in range(1, CH):
        serve(q)
    for dy in (1, 3, 2):
        to = join_index(x, z, lax.rem(y + dy, 4), c)
        remote(wbuf.at[0], wbuf.at[dy], ysend.at[dy], yrecv.at[dy], to).wait()
        shared_piece(dy)
    halves = [remote(sacc.at[1 + 2 * k], precv.at[k], psend.at[k], precv_sem.at[k], partner) for k in range(2)]
    for k in (1, 0):
        halves[k].start()

    def gather(q):
        first = 1 if q == 0 else 0
        bytes_of(back.at[pl.ds(q * PER + first, PER - first)], rrecv.at[q]).wait()
        rows = flat_rows(back[pl.ds(q * PER, PER)])
        at = lax.broadcasted_iota(I32, (TOK, TOK), 1) + q * TOK
        for k in range(2):
            part = dot((at == slot_col[k]).astype(F32).astype(BF), rows)
            if q == 0:
                pacc[k] = part
            else:
                pacc[k] = pacc[k] + part

    gather(0)
    halves[1].wait()
    xsend[...] = (sacc[2] + precv[1]).astype(BF)
    result = remote(xsend, xrecv, osend, orecv, across)
    result.start()
    halves[0].wait()
    rows_o[2] = (sacc[0] + precv[0]).astype(BF)
    for q in range(1, CH):
        gather(q)
    for k in range(2):
        rows_o[k] = pacc[k].astype(BF)
    bytes_of(lback.at[pl.ds(1, NEP - 1)], lrecv).wait()

    scores = lback[...].reshape(NEP, 128).astype(BF)
    lane = lax.broadcasted_iota(I32, (TOK, 128), 1)
    down_i = lax.broadcasted_iota(I32, (128, 128), 0)
    over_i = lax.broadcasted_iota(I32, (128, 128), 1)
    logits = slog[...]
    keep = jnp.ones((TOK, 128), F32)
    for k in range(2):
        col = slot_col[k]
        kept = col >= 0
        spot = jnp.where(kept, col // 8, -1)
        mine = dot((lane == spot).astype(F32).astype(BF), scores)
        mine = jnp.where(lane // 16 == jnp.where(kept, col % 8, -1), mine, 0.0).astype(BF)
        spread = jnp.logical_and(down_i % 16 == over_i % 16, (over_i // 16) % 4 == k)
        logits = logits + dot(mine, spread.astype(F32).astype(BF))
        keep = jnp.where((lane // 16) % 4 == k, kept.astype(F32), keep)
    values = keep * jax.nn.sigmoid(logits)
    pair = values + pltpu.roll(values, 16, 1)
    w_o[...] = values / (pair + pltpu.roll(pair, 32, 1))

    result.wait()
    rows_o[3] = xrecv[...]
    bytes_of(snd.at[pl.ds(1, NEP - 1)], dsend).wait()
    bytes_of(ret.at[pl.ds(1, NEP - 1)], rsend).wait()
    bytes_of(lret.at[pl.ds(1, NEP - 1)], lsend).wait()
    bytes_of(wbuf.at[0, pl.ds(1, 7)], zsend).wait()


def mix(rows_r, w_r, out_r):
    w = w_r[...]
    rows = [rows_r[i].astype(F32) for i in range(4)]
    for s in range(TASKS):
        acc = w[:, s : s + 1] * rows[0]
        for i in range(1, 4):
            acc = acc + w[:, 16 * i + s : 16 * i + s + 1] * rows[i]
        out_r[s] = acc.astype(BF)


def on_device(tokens, routes, capacity, expert_in, expert_out, shared_in, shared_out, route_gate, shared_gate):
    any_space = pl.BlockSpec(memory_space=pltpu.HBM)
    vmem = pl.BlockSpec(memory_space=pltpu.VMEM)
    dma = pltpu.SemaphoreType.DMA
    rows, weights = pl.pallas_call(
        exchange,
        out_shape=(
            jax.ShapeDtypeStruct((4, TOK, D), BF),
            jax.ShapeDtypeStruct((TOK, 128), F32),
        ),
        in_specs=[any_space] * 9,
        out_specs=(vmem, vmem),
        scratch_shapes=[
            pltpu.VMEM((2, TOK), I32),
            pltpu.VMEM((1, NEP), I32),
            pltpu.VMEM((1, TASKS * D), BF),
            pltpu.VMEM((2, TASKS * D), BF),
            pltpu.VMEM((D, H), BF),
            pltpu.VMEM((H, D), BF),
            pltpu.VMEM((2, 16, D), BF),
            pltpu.VMEM((4, 8, 2, 2, 16, D), BF),
            pltpu.VMEM((4, TOK, D), BF),
            pltpu.VMEM((NEP, 8, D), BF),
            pltpu.VMEM((NEP, 8, D), BF),
            pltpu.VMEM((NEP, 8, D), BF),
            pltpu.VMEM((NEP, 8, D), BF),
            pltpu.VMEM((NEP, 1, 128), F32),
            pltpu.VMEM((NEP, 1, 128), F32),
            pltpu.VMEM((4, TOK, D), F32),
            pltpu.VMEM((2, TOK, D), F32),
            pltpu.VMEM((TOK, D), BF),
            pltpu.VMEM((TOK, D), BF),
            pltpu.VMEM((2, TOK, D), F32),
            pltpu.VMEM((TOK, 128), F32),
            dma((9,)),
            dma((2,)),
            dma, dma((CH,)),
            dma, dma((CH,)),
            dma, dma,
            dma((4,)), dma((4,)),
            dma((2,)), dma((2,)),
            dma, dma,
            dma((4,)), dma((4,)),
            dma((2,)), dma((2,)),
            dma, dma,
        ],
        compiler_params=pltpu.CompilerParams(collective_id=0, has_side_effects=True, vmem_limit_bytes=63_000_000),
        name="exchange",
    )(
        tokens, routes.T, capacity.reshape(1, NEP), expert_in, expert_out,
        shared_in, shared_out, route_gate, shared_gate,
    )
    block = 32
    mixed = pl.pallas_call(
        mix,
        out_shape=jax.ShapeDtypeStruct((TASKS, TOK, D), BF),
        grid=(TOK // block,),
        in_specs=[
            pl.BlockSpec((4, block, D), lambda i: (0, i, 0)),
            pl.BlockSpec((block, 128), lambda i: (i, 0)),
        ],
        out_specs=pl.BlockSpec((TASKS, block, D), lambda i: (0, i, 0)),
        name="mix",
    )(rows, weights)
    return mixed.transpose(1, 0, 2)


def solution(mesh):
    rows, experts = P(("dp", "ep"), None), P("ep", None, None)
    return jax.shard_map(
        on_device,
        mesh=mesh,
        in_specs=(rows, rows, P(), experts, experts, P(None, "ep", None), P(None, "ep", None), P("ep", None), P()),
        out_specs=P(("dp", "ep"), None, None),
        check_vma=False,
    )
```

time: 265 us -> 94.8 us (0.36)
  the two profiles are of different devices: /device:TPU:1 before, /device:TPU:56 now
where the time goes in v1:
time: 94.8 us; the launch traced here: 94.6 us
  Pallas kernels  94.6 us (100%)
    pallas_call x1, Pallas kernels, on_device(): pl.pallas_call(exchange, out_shape=(jax.ShapeDtypeStruct((4, TOK, D), BF)...  87.6 us
    pallas_call x1, Pallas kernels, on_device(): pl.pallas_call(mix, out_shape=jax.ShapeDtypeStruct((TASKS, TOK, D), BF),...  6.91 us

profile of v1, /device:TPU:56, one launch (start us, length us, event | category | flops | bytes accessed | tf_op | source)
XLA Modules:
  0.0 94.6 jit_solution(7198116005694040071)
XLA Ops:
  0.0 87.6 %exchange.1 = (bf16[4,256,512]{2,1,0:T(8,128)(2,1)}, f32[256,128]{1,0:T(8,128)}) custom-call(bf16[256,512]{1,0:T(8,128)(2,1)} %tok_h.1, s32[2,256]{1,0:T(2,128)} %bitcast.3, s32[1,128]{1,0:T(1,128)} %bitcast.4, bf16[1,512,2048]{2,1,0:T(8,128)(2,1)} %ein_h.1, bf16[1,2048,512]{2,1,0:T(8,128)(2,1)} %eout_h.1, bf16[2,16,512]{2,1,0:T(8,128)(2,1)} %sin_h.1, ...), custom_call_target="tpu_custom_call" | custom-call | tf_op jit(solution)/shard_map/exchange/pallas_call | solution.py:328
  87.7 6.9 %mix.1 = bf16[12,256,512]{2,1,0:T(8,128)(2,1)} custom-call(bf16[4,256,512]{2,1,0:T(8,128)(2,1)} %get-tuple-element.7.rows_r, f32[256,128]{1,0:T(8,128)} %get-tuple-element.8.w_r), custom_call_target="tpu_custom_call" | custom-call | tf_op jit(solution)/shard_map/mix/pallas_call | solution.py:377

commit v2 on v1

v2 whole, which is shorter than its diff:
```python
import jax
import jax.numpy as jnp
from jax import lax
from jax.experimental import pallas as pl
from jax.experimental.pallas import tpu as pltpu
from jax.sharding import PartitionSpec as P

BF = jnp.bfloat16
F32 = jnp.float32
I32 = jnp.int32
MESH = pl.DeviceIdType.MESH
D = 512
H = 2048
TASKS = 12
TOK = 256
NEP = 128
CH = 4
PER = NEP // CH
SELF = 2 * PER


ZSTEP = (0, 1, 7, 2, 6, 3, 5, 4)
PARTS = ((0, 1), (1, 4), (5, 3))


def gelu(x):
    return jax.nn.gelu(x, approximate=True)


def dot(a, b, dims=((1,), (0,))):
    return lax.dot_general(a, b, (dims, ((), ())), preferred_element_type=F32)


def flat_rows(blocks):
    return blocks.astype(F32).reshape(-1, D).astype(BF)


def block_rows(rows):
    return rows.reshape(-1, 8, D).astype(BF)


def gate_tile(rows, group):
    sub = lax.broadcasted_iota(I32, (16, D), 0)
    tiles = []
    for row in rows:
        tile = jnp.zeros((16, D), F32)
        for s in range(TASKS):
            tile = jnp.where(sub == s, row[:, s * D : (s + 1) * D], tile)
        tiles.append(tile)
    zero = jnp.zeros((16, D), F32)
    picked = [zero if group(g) is None else tiles[group(g)] for g in range(8)]
    return jnp.concatenate(picked, axis=0).astype(BF)


def exchange(
    tok_h, routes_h, cap_h, ein_h, eout_h, sin_h, sout_h, rg_h, sg_h,
    rows_o, w_o,
    routes_v, cap_v, rg_v, sg_v, ein_v, eout_v, xs, wbuf, tokq,
    snd, recv, ret, back, lret, lback, sacc, precv, xsend, xrecv, pacc, slog,
    load_sem, big_sem, dsend, drecv, rsend, rrecv, lsend, lrecv,
    tsend, trecv, xssem, xrsem, zsend, zrecv, ysend, yrecv, psend, precv_sem, osend, orecv, csend, crecv,
):
    me = lax.axis_index("ep")
    x, z, y, c = me >> 6, (me >> 3) & 7, (me >> 1) & 3, me & 1
    d = lax.axis_index("dp")
    mine = x ^ d
    xpart = [x * 64, (1 - x) * 64]
    zpart = [((z + d) & 7) * 8 for d in range(8)]
    cpart = [c, 1 - c]

    def load(src, dst, k):
        return pltpu.make_async_copy(src, dst, load_sem.at[k])

    loads = [
        load(routes_h, routes_v, 0),
        load(cap_h, cap_v, 1),
        load(tok_h, tokq.at[0], 2),
        load(rg_h, rg_v, 3),
        load(sg_h, sg_v, 4),
        load(sin_h, xs.at[0], 5),
        load(sout_h, xs.at[1], 6),
    ]
    for k in loads:
        k.start()
    big = [
        pltpu.make_async_copy(ein_h.at[0], ein_v, big_sem.at[0]),
        pltpu.make_async_copy(eout_h.at[0], eout_v, big_sem.at[1]),
    ]
    for k in big:
        k.start()

    barrier = pltpu.get_barrier_semaphore()
    other = {"dp": 1 - d, "ep": xpart[1] + (me & 63)}
    pl.semaphore_signal(barrier, inc=1, device_id=other, device_id_type=MESH)
    for dz in (4, 3, 5, 2, 6, 1, 7, 0):
        for dy in (2, 1, 3, 0):
            for dx in (1, 0):
                for dc in (1, 0):
                    if dz or dy or dx or dc:
                        to = xpart[dx] + zpart[dz] + ((y + dy) & 3) * 2 + cpart[dc]
                        pl.semaphore_signal(barrier, inc=1, device_id={"ep": to}, device_id_type=MESH)

    with jax.named_scope("loadwait"):
        for k in loads:
            k.wait()

    expert = lax.broadcasted_iota(I32, (NEP, 1), 0)
    dz = ((expert >> 3) - z + 8) & 7
    zi = jnp.where(dz == 0, 0, jnp.where(dz <= 4, 2 * dz - 1, 2 * (8 - dz)))
    place = (((((expert - c + 2) & 1) + 2 - 2 * (((expert >> 6) - x + 2) & 1)) * 4) + (((expert >> 1) - y + 4) & 3)) * 8 + zi
    base = (place * 8).astype(F32)
    named = lax.broadcasted_iota(I32, (NEP, TOK), 0)
    chosen = [(named == routes_v[k : k + 1, :]).astype(F32) for k in range(2)]
    earlier = (
        lax.broadcasted_iota(I32, (TOK, TOK), 0) < lax.broadcasted_iota(I32, (TOK, TOK), 1)
    ).astype(BF)
    before = dot((chosen[0] + chosen[1]).astype(BF), earlier)
    cap = jnp.broadcast_to(cap_v[...].astype(F32), (8, NEP)).astype(BF)
    slots = []
    for k in range(2):
        rank = jnp.sum(chosen[k] * before, axis=0, keepdims=True)
        start = jnp.sum(chosen[k] * base, axis=0, keepdims=True)
        limit = dot(cap, chosen[k].astype(BF))[0:1]
        slots.append(jnp.where(rank < limit, start + rank, -1.0))
    slot_row = [s.astype(I32) for s in slots]
    slot_col = [
        jnp.transpose(jnp.broadcast_to(s, (128, TOK)))[:, 0:1].astype(I32) for s in slots
    ]

    own = tokq[0]
    for q in range(CH):
        at = lax.broadcasted_iota(I32, (TOK, TOK), 0) + q * TOK
        pick = jnp.logical_or(at == slot_row[0], at == slot_row[1]).astype(F32).astype(BF)
        rows = block_rows(dot(pick, own))
        snd[pl.ds(q * PER, PER)] = rows
        if q == SELF // PER:
            recv[SELF : SELF + 1] = rows[0:1]

    wbuf[d, 0, 0, x] = xs[d, mine]
    gates = gate_tile([rg_v[...].astype(F32)], lambda g: 0)
    sg = sg_v[...].astype(F32)
    sg_own = jnp.where(mine == 0, sg[0:1], sg[1:2])
    sg_other = jnp.where(mine == 0, sg[1:2], sg[0:1])
    shared_gates = gate_tile([sg_own, sg_other], lambda g: g % 4 - 2 if g % 4 >= 2 else None)
    slog[...] = dot(own, shared_gates, ((1,), (1,))).astype(BF).astype(F32)

    with jax.named_scope("barrier"):
        pl.semaphore_wait(barrier, NEP)

    def remote(src, dst, ss, rs, to):
        return pltpu.make_async_remote_copy(
            src_ref=src, dst_ref=dst, send_sem=ss, recv_sem=rs,
            device_id=to if isinstance(to, dict) else {"ep": to}, device_id_type=MESH,
        )

    def bytes_of(a, sem):
        return pltpu.make_async_copy(a, a, sem)

    def toward(dx, dz, dy, dc):
        return xpart[dx] + zpart[dz] + ((y + dy) & 3) * 2 + cpart[dc]

    def each(q, low, high, sign, act):
        dx, dc = 1 - q // 2, q % 2
        if q == SELF // PER and low == 0:
            for i in range(1, 8):
                act(SELF + i, toward(dx, sign * ZSTEP[i] % 8, 0, dc))
            low = 1

        @pl.loop(low, high)
        def _(dy):
            for i in range(8):
                act(q * PER + dy * 8 + i, toward(dx, sign * ZSTEP[i] % 8, 4 + sign * dy, dc))

    across = toward(1, 0, 0, 0)
    partner = toward(0, 0, 0, 1)

    def dispatch(q, low=0, high=4):
        each(q, low, high, 1, lambda n, to: remote(snd.at[n], recv.at[n], dsend, drecv.at[q], to).start())

    x_half = remote(xs.at[d, 1 - mine], wbuf.at[d, 0, 0, x], xssem, xrsem, across)
    x_half.start()
    dispatch(0, 0, 2)
    with jax.named_scope("xwait"):
        x_half.wait()

    def along_z(src, slot, k, dz):
        return remote(src, wbuf.at[(d, 0) + slot], zsend.at[k], zrecv.at[k], toward(0, dz, 0, 0))

    near = [along_z(wbuf.at[d, 0, 0], (i,), i, ZSTEP[i]) for i in (1, 2, 3, 4)]
    far = [
        along_z(wbuf.at[d, 0, 3], (5,), 5, 1),
        along_z(wbuf.at[d, 0, 4], (6,), 6, 7),
        along_z(wbuf.at[d, 0, 3, 0], (7, 0), 0, 2),
        along_z(wbuf.at[d, 0, 4, 1], (7, 1), 7, 6),
    ]
    along_y = []
    for j, (first, count) in enumerate(PARTS):
        along_y.append({
            dy: remote(
                wbuf.at[d, 0, pl.ds(first, count)], wbuf.at[d, dy, pl.ds(first, count)],
                ysend.at[dy, j], yrecv.at[dy, j], toward(0, 0, dy, 0),
            )
            for dy in (1, 3, 2)
        })
    swap = [remote(wbuf.at[d, p], wbuf.at[d, p], csend.at[p], crecv.at[p], other) for p in range(4)]
    quad = [
        remote(tokq.at[0], tokq.at[p], tsend.at[p], trecv.at[p], to)
        for p, to in ((1, partner), (2, across))
    ]
    passed_on = remote(tokq.at[2], tokq.at[3], tsend.at[3], trecv.at[3], partner)

    for k in near:
        k.start()
    for k in along_y[0].values():
        k.start()
    dispatch(0, 2, 4)
    with jax.named_scope("nearwait"):
        for k in near:
            k.wait_recv()
    for k in far:
        k.start()
    for k in along_y[1].values():
        k.start()
    with jax.named_scope("dispatch123"):
        dispatch(1)
        for k in quad:
            k.start()
        dispatch(2)
        dispatch(3)
    for k in big:
        k.wait()

    fold = (
        lax.broadcasted_iota(I32, (TOK, 128), 1) // 16 == lax.broadcasted_iota(I32, (TOK, 128), 0) % 8
    )

    def serve(q):
        first = 1 if q == SELF // PER else 0
        with jax.named_scope("dwait"):
            bytes_of(recv.at[pl.ds(q * PER + first, PER - first)], drecv.at[q]).wait()
        rows = flat_rows(recv[pl.ds(q * PER, PER)])
        scores = dot(rows, gates, ((1,), (1,))).astype(BF).astype(F32)
        scores = jnp.sum(
            jnp.where(fold, scores, 0.0).reshape(PER, 8, 128), axis=1, keepdims=True
        )
        lret[pl.ds(q * PER, PER)] = scores
        if q == SELF // PER:
            lback[SELF : SELF + 1] = scores[0:1]
        total = jnp.zeros((TOK, D), F32)
        for t in range(4):
            hidden = gelu(dot(rows, ein_v[:, t * 512 : (t + 1) * 512])).astype(BF)
            total = total + dot(hidden, eout_v[t * 512 : (t + 1) * 512, :])
        made = block_rows(total)
        ret[pl.ds(q * PER, PER)] = made
        if q == SELF // PER:
            back[SELF : SELF + 1] = made[0:1]
        with jax.named_scope("logsend"):
            each(q, 0, 4, -1, lambda n, to: remote(lret.at[n], lback.at[n], lsend, lrecv, to).start())
        with jax.named_scope("retsend"):
            each(q, 0, 4, -1, lambda n, to: remote(ret.at[n], back.at[n], rsend, rrecv.at[q], to).start())

    def shared_block(p, b, up, down):
        hidden = gelu(dot(tokq[b], up, ((1,), (1,)))).astype(BF)
        part = dot(hidden, down)
        if p == 0:
            sacc[b] = part
        else:
            sacc[b] = sacc[b] + part

    def shared_weights(p):
        with jax.named_scope("swapwait"):
            swap[p].wait()
        return wbuf[0, p].reshape(256, D), wbuf[1, p].reshape(256, D)

    def shared_piece(p):
        up, down = shared_weights(p)

        @pl.loop(0, 4)
        def _(b):
            shared_block(p, b, up, down)

    def y_arrived(dy):
        with jax.named_scope("ywait"):
            for part in along_y:
                part[dy].wait()
        swap[dy].start()

    serve(0)
    with jax.named_scope("farwait"):
        for k in far:
            k.wait_recv()
    for k in along_y[2].values():
        k.start()
    swap[0].start()
    serve(1)
    with jax.named_scope("quadwait"):
        for k in quad:
            k.wait()
        passed_on.start()
    y_arrived(1)
    y_arrived(3)
    serve(2)
    passed_on.wait()
    shared_piece(0)
    y_arrived(2)
    serve(3)
    shared_piece(1)
    shared_piece(3)
    up, down = shared_weights(2)
    halves = [remote(sacc.at[1 + 2 * k], precv.at[k], psend.at[k], precv_sem.at[k], partner) for k in range(2)]
    result = remote(xsend, xrecv, osend, orecv, across)
    shared_block(2, 3, up, down)
    halves[1].start()
    shared_block(2, 1, up, down)
    halves[0].start()
    shared_block(2, 2, up, down)
    with jax.named_scope("h1wait"):
        halves[1].wait()
    xsend[...] = (sacc[2] + precv[1]).astype(BF)
    result.start()
    shared_block(2, 0, up, down)
    with jax.named_scope("h0wait"):
        halves[0].wait()
    rows_o[2] = (sacc[0] + precv[0]).astype(BF)

    def gather(q):
        first = 1 if q == SELF // PER else 0
        with jax.named_scope("rwait"):
            bytes_of(back.at[pl.ds(q * PER + first, PER - first)], rrecv.at[q]).wait()
        rows = flat_rows(back[pl.ds(q * PER, PER)])
        at = lax.broadcasted_iota(I32, (TOK, TOK), 1) + q * TOK
        for k in range(2):
            part = dot((at == slot_col[k]).astype(F32).astype(BF), rows)
            if q == 0:
                pacc[k] = part
            elif q < CH - 1:
                pacc[k] = pacc[k] + part
            else:
                rows_o[k] = (pacc[k] + part).astype(BF)

    for q in range(CH - 1):
        gather(q)
    with jax.named_scope("lwait"):
        bytes_of(lback.at[pl.ds(1, NEP - 1)], lrecv).wait()

    scores = lback[...].reshape(NEP, 128).astype(BF)
    lane = lax.broadcasted_iota(I32, (TOK, 128), 1)
    down_i = lax.broadcasted_iota(I32, (128, 128), 0)
    over_i = lax.broadcasted_iota(I32, (128, 128), 1)
    logits = slog[...]
    keep = jnp.ones((TOK, 128), F32)
    for k in range(2):
        col = slot_col[k]
        kept = col >= 0
        spot = jnp.where(kept, col // 8, -1)
        mine = dot((lane == spot).astype(F32).astype(BF), scores)
        mine = jnp.where(lane // 16 == jnp.where(kept, col % 8, -1), mine, 0.0).astype(BF)
        spread = jnp.logical_and(down_i % 16 == over_i % 16, (over_i // 16) % 4 == k)
        logits = logits + dot(mine, spread.astype(F32).astype(BF))
        keep = jnp.where((lane // 16) % 4 == k, kept.astype(F32), keep)
    values = keep * jax.nn.sigmoid(logits)
    pair = values + pltpu.roll(values, 16, 1)
    w_o[...] = values / (pair + pltpu.roll(pair, 32, 1))

    with jax.named_scope("owait"):
        result.wait()
    rows_o[3] = xrecv[...]
    gather(CH - 1)
    for k in near + far:
        k.wait_send()
    bytes_of(snd.at[pl.ds(1, NEP - 1)], dsend).wait()
    bytes_of(lret.at[pl.ds(1, NEP - 1)], lsend).wait()
    bytes_of(ret.at[pl.ds(1, NEP - 1)], rsend).wait()


TB = 32
OUT_PARTS = 8


def mix(rows_r, w_r, out_h, buf, sem):
    wide = 4 * TB
    w = w_r[...]
    high = w.astype(BF)
    lane = lax.broadcasted_iota(I32, (128, TASKS * wide), 1)
    row = lax.broadcasted_iota(I32, (128, TASKS * wide), 0)
    take = (row == (lane % wide) // TB * 16 + lane // wide).astype(F32).astype(BF)
    diagonal = (
        lax.broadcasted_iota(I32, (TOK, wide), 1) % TB == lax.broadcasted_iota(I32, (TOK, wide), 0) % TB
    )
    planes = []
    for source in (high, (w - high.astype(F32)).astype(BF)):
        spread = dot(source, take)
        planes.append([
            jnp.where(diagonal, spread[:, s * wide : (s + 1) * wide], 0.0).astype(BF) for s in range(TASKS)
        ])
    size = TOK // OUT_PARTS

    def put(h):
        at = pl.ds(h * size, size)
        return pltpu.make_async_copy(buf.at[:, at], out_h.at[:, at], sem.at[h])

    for b in range(TOK // TB):
        at = slice(b * TB, (b + 1) * TB)
        terms = jnp.concatenate([rows_r[i, at] for i in range(4)] * 2, axis=0)
        left = jnp.concatenate(
            [jnp.concatenate([planes[0][s][at] for s in range(TASKS)], axis=0),
             jnp.concatenate([planes[1][s][at] for s in range(TASKS)], axis=0)], axis=1)
        made = dot(left, terms).astype(BF)
        for s in range(TASKS):
            buf[s, at] = made[s * TB : (s + 1) * TB]
        if (b + 1) * TB % size == 0:
            put((b + 1) * TB // size - 1).start()
    for h in range(OUT_PARTS):
        put(h).wait()


def on_device(tokens, routes, capacity, expert_in, expert_out, shared_in, shared_out, route_gate, shared_gate):
    hbm = pl.BlockSpec(memory_space=pltpu.HBM)
    vmem = pl.BlockSpec(memory_space=pltpu.VMEM)
    dma = pltpu.SemaphoreType.DMA
    rows, weights = pl.pallas_call(
        exchange,
        out_shape=(
            jax.ShapeDtypeStruct((4, TOK, D), BF),
            jax.ShapeDtypeStruct((TOK, 128), F32),
        ),
        in_specs=[hbm] * 9,
        out_specs=(vmem, vmem),
        scratch_shapes=[
            pltpu.VMEM((2, TOK), I32),
            pltpu.VMEM((1, NEP), I32),
            pltpu.VMEM((1, TASKS * D), BF),
            pltpu.VMEM((2, TASKS * D), BF),
            pltpu.VMEM((D, H), BF),
            pltpu.VMEM((H, D), BF),
            pltpu.VMEM((2, 2, 16, D), BF),
            pltpu.VMEM((2, 4, 8, 2, 16, D), BF),
            pltpu.VMEM((4, TOK, D), BF),
            pltpu.VMEM((NEP, 8, D), BF),
            pltpu.VMEM((NEP, 8, D), BF),
            pltpu.VMEM((NEP, 8, D), BF),
            pltpu.VMEM((NEP, 8, D), BF),
            pltpu.VMEM((NEP, 1, 128), F32),
            pltpu.VMEM((NEP, 1, 128), F32),
            pltpu.VMEM((4, TOK, D), F32),
            pltpu.VMEM((2, TOK, D), F32),
            pltpu.VMEM((TOK, D), BF),
            pltpu.VMEM((TOK, D), BF),
            pltpu.VMEM((2, TOK, D), F32),
            pltpu.VMEM((TOK, 128), F32),
            dma((7,)),
            dma((2,)),
            dma, dma((CH,)),
            dma, dma((CH,)),
            dma, dma,
            dma((4,)), dma((4,)),
            dma, dma,
            dma((8,)), dma((8,)),
            dma((4, 3)), dma((4, 3)),
            dma((2,)), dma((2,)),
            dma, dma,
            dma((4,)), dma((4,)),
        ],
        compiler_params=pltpu.CompilerParams(collective_id=0, has_side_effects=True, vmem_limit_bytes=40 * 2**20),
        name="exchange",
    )(*[
        pltpu.with_memory_space_constraint(a, pltpu.HBM)
        for a in (
            tokens, routes.T, capacity.reshape(1, NEP), expert_in, expert_out,
            shared_in, shared_out, route_gate, shared_gate,
        )
    ])
    mixed = pl.pallas_call(
        mix,
        out_shape=jax.ShapeDtypeStruct((TASKS, TOK, D), BF),
        in_specs=[vmem, vmem],
        out_specs=hbm,
        scratch_shapes=[pltpu.VMEM((TASKS, TOK, D), BF), dma((OUT_PARTS,))],
        compiler_params=pltpu.CompilerParams(vmem_limit_bytes=24 * 2**20),
        name="mix",
    )(rows, weights)
    return mixed.transpose(1, 0, 2)


def solution(mesh):
    rows, experts = P(("dp", "ep"), None), P("ep", None, None)
    return jax.shard_map(
        on_device,
        mesh=mesh,
        in_specs=(rows, rows, P(), experts, experts, P(None, "ep", None), P(None, "ep", None), P("ep", None), P()),
        out_specs=P(("dp", "ep"), None, None),
        check_vma=False,
    )
```

time: 94.8 us -> 69.5 us (0.73)
  the two profiles are of different devices: /device:TPU:56 before, /device:TPU:1 now
where the time goes in v2:
time: 69.5 us
  Pallas kernels  69.5 us (100%)
    pallas_call x1, Pallas kernels, on_device(): pl.pallas_call(exchange, out_shape=(jax.ShapeDtypeStruct((4, TOK, D), BF)...  67 us
    pallas_call x1, Pallas kernels, on_device(): pl.pallas_call(mix, out_shape=jax.ShapeDtypeStruct((TASKS, TOK, D), BF),...  2.42 us

profile of v2, /device:TPU:1, one launch (start us, length us, event | category | flops | bytes accessed | tf_op | source)
XLA Modules:
  0.0 69.5 jit_solution(9818436091802192127)
XLA Ops:
  0.0 67.0 %exchange.1 = (bf16[4,256,512]{2,1,0:T(8,128)(2,1)S(1)}, f32[256,128]{1,0:T(8,128)S(1)}) custom-call(bf16[256,512]{1,0:T(8,128)(2,1)} %tok_h.1, s32[2,256]{1,0:T(2,128)} %bitcast.3, s32[1,128]{1,0:T(1,128)} %bitcast.4, bf16[1,512,2048]{2,1,0:T(8,128)(2,1)} %ein_h.1, bf16[1,2048,512]{2,1,0:T(8,128)(2,1)} %eout_h.1, bf16[2,16,512]{2,1,0:T(8,128)(2,1)} %sin_h.1, ...), custom_call_target="tpu_custom_call" | custom-call | tf_op jit(solution)/shard_map/exchange/pallas_call | solution.py:421
  67.1 2.4 %mix.1 = bf16[12,256,512]{2,1,0:T(8,128)(2,1)} custom-call(bf16[4,256,512]{2,1,0:T(8,128)(2,1)S(1)} %get-tuple-element.7.rows_r, f32[256,128]{1,0:T(8,128)S(1)} %get-tuple-element.8.w_r), custom_call_target="tpu_custom_call" | custom-call | tf_op jit(solution)/shard_map/mix/pallas_call | solution.py:473

commit v3 on v2

--- a/solution.py
+++ b/solution.py
@@ -19,6 +19,7 @@
 SELF = 2 * PER
 
 
+TB = 32
 ZSTEP = (0, 1, 7, 2, 6, 3, 5, 4)
 PARTS = ((0, 1), (1, 4), (5, 3))
 
@@ -77,11 +78,11 @@
         load(tok_h, tokq.at[0], 2),
         load(rg_h, rg_v, 3),
         load(sg_h, sg_v, 4),
-        load(sin_h, xs.at[0], 5),
-        load(sout_h, xs.at[1], 6),
     ]
     for k in loads:
         k.start()
+    load(sin_h, xs.at[0], 5).start()
+    load(sout_h, xs.at[1], 5).start()
     big = [
         pltpu.make_async_copy(ein_h.at[0], ein_v, big_sem.at[0]),
         pltpu.make_async_copy(eout_h.at[0], eout_v, big_sem.at[1]),
@@ -103,6 +104,7 @@
     with jax.named_scope("loadwait"):
         for k in loads:
             k.wait()
+        load(xs, xs, 5).wait()
 
     expert = lax.broadcasted_iota(I32, (NEP, 1), 0)
     dz = ((expert >> 3) - z + 8) & 7
@@ -184,49 +186,71 @@
         x_half.wait()
 
     def along_z(src, slot, k, dz):
-        return remote(src, wbuf.at[(d, 0) + slot], zsend.at[k], zrecv.at[k], toward(0, dz, 0, 0))
-
-    near = [along_z(wbuf.at[d, 0, 0], (i,), i, ZSTEP[i]) for i in (1, 2, 3, 4)]
+        return remote(src, wbuf.at[(d, 0) + slot], zsend, zrecv.at[k], toward(0, dz, 0, 0))
+
+    near = [along_z(wbuf.at[d, 0, 0], (i,), 0, ZSTEP[i]) for i in (1, 2, 3, 4)]
     far = [
-        along_z(wbuf.at[d, 0, 3], (5,), 5, 1),
-        along_z(wbuf.at[d, 0, 4], (6,), 6, 7),
-        along_z(wbuf.at[d, 0, 3, 0], (7, 0), 0, 2),
-        along_z(wbuf.at[d, 0, 4, 1], (7, 1), 7, 6),
+        along_z(wbuf.at[d, 0, 3], (5,), 1, 1),
+        along_z(wbuf.at[d, 0, 4], (6,), 1, 7),
+        along_z(wbuf.at[d, 0, 3, 0], (7, 0), 1, 2),
+        along_z(wbuf.at[d, 0, 4, 1], (7, 1), 1, 6),
     ]
     along_y = []
     for j, (first, count) in enumerate(PARTS):
         along_y.append({
             dy: remote(
                 wbuf.at[d, 0, pl.ds(first, count)], wbuf.at[d, dy, pl.ds(first, count)],
-                ysend.at[dy, j], yrecv.at[dy, j], toward(0, 0, dy, 0),
+                ysend, yrecv.at[j], toward(0, 0, dy, 0),
             )
             for dy in (1, 3, 2)
         })
-    swap = [remote(wbuf.at[d, p], wbuf.at[d, p], csend.at[p], crecv.at[p], other) for p in range(4)]
+    swap = []
+    for j, (first, count) in enumerate(PARTS):
+        swap.append([
+            remote(
+                wbuf.at[d, p, pl.ds(first, count)], wbuf.at[d, p, pl.ds(first, count)],
+                csend, crecv.at[p], other,
+            )
+            for p in range(4)
+        ])
     quad = [
-        remote(tokq.at[0], tokq.at[p], tsend.at[p], trecv.at[p], to)
+        remote(tokq.at[0], tokq.at[p], tsend, trecv.at[0], to)
         for p, to in ((1, partner), (2, across))
     ]
-    passed_on = remote(tokq.at[2], tokq.at[3], tsend.at[3], trecv.at[3], partner)
+    passed_on = remote(tokq.at[2], tokq.at[3], tsend, trecv.at[1], partner)
+
+    def y_arrived(j):
+        with jax.named_scope("ywait"):
+            first, count = PARTS[j]
+            bytes_of(wbuf.at[d, pl.ds(1, 3), pl.ds(first, count)], yrecv.at[j]).wait()
+        for dy in (1, 3, 2):
+            swap[j][dy].start()
 
     for k in near:
         k.start()
     for k in along_y[0].values():
         k.start()
+    swap[0][0].start()
     dispatch(0, 2, 4)
+    dispatch(1, 0, 2)
     with jax.named_scope("nearwait"):
-        for k in near:
-            k.wait_recv()
+        bytes_of(wbuf.at[d, 0, pl.ds(1, 4)], zrecv.at[0]).wait()
     for k in far:
         k.start()
     for k in along_y[1].values():
         k.start()
-    with jax.named_scope("dispatch123"):
-        dispatch(1)
-        for k in quad:
-            k.start()
-        dispatch(2)
-        dispatch(3)
+    swap[1][0].start()
+    dispatch(1, 2, 4)
+    for k in quad:
+        k.start()
+    with jax.named_scope("farwait"):
+        bytes_of(wbuf.at[d, 0, pl.ds(5, 3)], zrecv.at[1]).wait()
+    for k in along_y[2].values():
+        k.start()
+    swap[2][0].start()
+    dispatch(2)
+    dispatch(3)
+    y_arrived(0)
     for k in big:
         k.wait()
 
@@ -257,7 +281,14 @@
         with jax.named_scope("logsend"):
             each(q, 0, 4, -1, lambda n, to: remote(lret.at[n], lback.at[n], lsend, lrecv, to).start())
         with jax.named_scope("retsend"):
-            each(q, 0, 4, -1, lambda n, to: remote(ret.at[n], back.at[n], rsend, rrecv.at[q], to).start())
+            if q < CH - 1:
+                each(q, 0, 4, -1, lambda n, to: remote(ret.at[n], back.at[n], rsend, rrecv.at[q], to).start())
+            else:
+                for i in (7, 6, 5, 4, 3, 2, 1, 0):
+                    for dy in (2, 1, 3, 0):
+                        n = q * PER + dy * 8 + i
+                        to = toward(1 - q // 2, -ZSTEP[i] % 8, 4 - dy, q % 2)
+                        remote(ret.at[n], back.at[n], rsend, rrecv.at[q], to).start()
 
     def shared_block(p, b, up, down):
         hidden = gelu(dot(tokq[b], up, ((1,), (1,)))).astype(BF)
@@ -269,7 +300,7 @@
 
     def shared_weights(p):
         with jax.named_scope("swapwait"):
-            swap[p].wait()
+            bytes_of(wbuf.at[1 - d, p], crecv.at[p]).wait()
         return wbuf[0, p].reshape(256, D), wbuf[1, p].reshape(256, D)
 
     def shared_piece(p):
@@ -279,35 +310,21 @@
         def _(b):
             shared_block(p, b, up, down)
 
-    def y_arrived(dy):
-        with jax.named_scope("ywait"):
-            for part in along_y:
-                part[dy].wait()
-        swap[dy].start()
-
     serve(0)
-    with jax.named_scope("farwait"):
-        for k in far:
-            k.wait_recv()
-    for k in along_y[2].values():
-        k.start()
-    swap[0].start()
+    y_arrived(1)
     serve(1)
     with jax.named_scope("quadwait"):
-        for k in quad:
-            k.wait()
+        bytes_of(tokq.at[pl.ds(1, 2)], trecv.at[0]).wait()
         passed_on.start()
-    y_arrived(1)
-    y_arrived(3)
+    y_arrived(2)
     serve(2)
-    passed_on.wait()
+    passed_on.wait_recv()
     shared_piece(0)
-    y_arrived(2)
     serve(3)
     shared_piece(1)
     shared_piece(3)
     up, down = shared_weights(2)
-    halves = [remote(sacc.at[1 + 2 * k], precv.at[k], psend.at[k], precv_sem.at[k], partner) for k in range(2)]
+    halves = [remote(sacc.at[1 + 2 * k], precv.at[k], psend, precv_sem.at[k], partner) for k in range(2)]
     result = remote(xsend, xrecv, osend, orecv, across)
     shared_block(2, 3, up, down)
     halves[1].start()
@@ -315,12 +332,12 @@
     halves[0].start()
     shared_block(2, 2, up, down)
     with jax.named_scope("h1wait"):
-        halves[1].wait()
+        halves[1].wait_recv()
     xsend[...] = (sacc[2] + precv[1]).astype(BF)
     result.start()
     shared_block(2, 0, up, down)
     with jax.named_scope("h0wait"):
-        halves[0].wait()
+        halves[0].wait_recv()
     rows_o[2] = (sacc[0] + precv[0]).astype(BF)
 
     def gather(q):
@@ -360,39 +377,37 @@
         keep = jnp.where((lane // 16) % 4 == k, kept.astype(F32), keep)
     values = keep * jax.nn.sigmoid(logits)
     pair = values + pltpu.roll(values, 16, 1)
-    w_o[...] = values / (pair + pltpu.roll(pair, 32, 1))
+    weights = values / (pair + pltpu.roll(pair, 32, 1))
+    wide = 4 * TB
+    col = lax.broadcasted_iota(I32, (128, TASKS * wide), 1)
+    line = lax.broadcasted_iota(I32, (128, TASKS * wide), 0)
+    take = (line == (col % wide) // TB * 16 + col // wide).astype(F32).astype(BF)
+    diagonal = (
+        lax.broadcasted_iota(I32, (TOK, wide), 1) % TB == lax.broadcasted_iota(I32, (TOK, wide), 0) % TB
+    )
+    spread = dot(weights.astype(BF), take)
+    for s in range(TASKS):
+        w_o[s] = jnp.where(diagonal, spread[:, s * wide : (s + 1) * wide], 0.0).astype(BF)
 
     with jax.named_scope("owait"):
         result.wait()
     rows_o[3] = xrecv[...]
     gather(CH - 1)
-    for k in near + far:
-        k.wait_send()
-    bytes_of(snd.at[pl.ds(1, NEP - 1)], dsend).wait()
-    bytes_of(lret.at[pl.ds(1, NEP - 1)], lsend).wait()
-    bytes_of(ret.at[pl.ds(1, NEP - 1)], rsend).wait()
-
-
-TB = 32
+    with jax.named_scope("sendwait"):
+        bytes_of(wbuf.at[0, 0, pl.ds(1, 7)], zsend).wait()
+        bytes_of(wbuf.at[0, pl.ds(1, 3)], ysend).wait()
+        bytes_of(wbuf.at[0], csend).wait()
+        bytes_of(tokq.at[pl.ds(1, 3)], tsend).wait()
+        bytes_of(precv, psend).wait()
+        bytes_of(snd.at[pl.ds(1, NEP - 1)], dsend).wait()
+        bytes_of(lret.at[pl.ds(1, NEP - 1)], lsend).wait()
+        bytes_of(ret.at[pl.ds(1, NEP - 1)], rsend).wait()
+
+
 OUT_PARTS = 8
 
 
 def mix(rows_r, w_r, out_h, buf, sem):
-    wide = 4 * TB
-    w = w_r[...]
-    high = w.astype(BF)
-    lane = lax.broadcasted_iota(I32, (128, TASKS * wide), 1)
-    row = lax.broadcasted_iota(I32, (128, TASKS * wide), 0)
-    take = (row == (lane % wide) // TB * 16 + lane // wide).astype(F32).astype(BF)
-    diagonal = (
-        lax.broadcasted_iota(I32, (TOK, wide), 1) % TB == lax.broadcasted_iota(I32, (TOK, wide), 0) % TB
-    )
-    planes = []
-    for source in (high, (w - high.astype(F32)).astype(BF)):
-        spread = dot(source, take)
-        planes.append([
-            jnp.where(diagonal, spread[:, s * wide : (s + 1) * wide], 0.0).astype(BF) for s in range(TASKS)
-        ])
     size = TOK // OUT_PARTS
 
     def put(h):
@@ -401,10 +416,8 @@
 
     for b in range(TOK // TB):
         at = slice(b * TB, (b + 1) * TB)
-        terms = jnp.concatenate([rows_r[i, at] for i in range(4)] * 2, axis=0)
-        left = jnp.concatenate(
-            [jnp.concatenate([planes[0][s][at] for s in range(TASKS)], axis=0),
-             jnp.concatenate([planes[1][s][at] for s in range(TASKS)], axis=0)], axis=1)
+        terms = jnp.concatenate([rows_r[i, at] for i in range(4)], axis=0)
+        left = jnp.concatenate([w_r[s, at] for s in range(TASKS)], axis=0)
         made = dot(left, terms).astype(BF)
         for s in range(TASKS):
             buf[s, at] = made[s * TB : (s + 1) * TB]
@@ -422,7 +435,7 @@
         exchange,
         out_shape=(
             jax.ShapeDtypeStruct((4, TOK, D), BF),
-            jax.ShapeDtypeStruct((TOK, 128), F32),
+            jax.ShapeDtypeStruct((TASKS, TOK, 4 * TB), BF),
         ),
         in_specs=[hbm] * 9,
         out_specs=(vmem, vmem),
@@ -448,18 +461,18 @@
             pltpu.VMEM((TOK, D), BF),
             pltpu.VMEM((2, TOK, D), F32),
             pltpu.VMEM((TOK, 128), F32),
-            dma((7,)),
+            dma((6,)),
             dma((2,)),
             dma, dma((CH,)),
             dma, dma((CH,)),
             dma, dma,
-            dma((4,)), dma((4,)),
+            dma, dma((2,)),
             dma, dma,
-            dma((8,)), dma((8,)),
-            dma((4, 3)), dma((4, 3)),
-            dma((2,)), dma((2,)),
+            dma, dma((2,)),
+            dma, dma((3,)),
+            dma, dma((2,)),
             dma, dma,
-            dma((4,)), dma((4,)),
+            dma, dma((4,)),
         ],
         compiler_params=pltpu.CompilerParams(collective_id=0, has_side_effects=True, vmem_limit_bytes=40 * 2**20),
         name="exchange",

time: 69.5 us -> 66.5 us (0.957)
  Pallas kernels: 69.5 us -> 66.5 us
    pallas_call x1, Pallas kernels: 67 us -> 64.5 us  [on_device(): pl.pallas_call(exchange, out_shape=(jax.ShapeDtypeStruct((4, TOK, D), BF)...]
where the time goes in v3:
time: 66.5 us
  Pallas kernels  66.5 us (100%)
    pallas_call x1, Pallas kernels, on_device(): pl.pallas_call(exchange, out_shape=(jax.ShapeDtypeStruct((4, TOK, D), BF)...  64.5 us
    pallas_call x1, Pallas kernels, on_device(): pl.pallas_call(mix, out_shape=jax.ShapeDtypeStruct((TASKS, TOK, D), BF),...  1.97 us

profile of v3, /device:TPU:1, one launch (start us, length us, event | category | flops | bytes accessed | tf_op | source)
XLA Modules:
  0.0 66.5 jit_solution(3959690141302502442)
XLA Ops:
  0.0 64.5 %exchange.1 = (bf16[4,256,512]{2,1,0:T(8,128)(2,1)S(1)}, bf16[12,256,128]{2,1,0:T(8,128)(2,1)S(1)}) custom-call(bf16[256,512]{1,0:T(8,128)(2,1)} %tok_h.1, s32[2,256]{1,0:T(2,128)} %bitcast.3, s32[1,128]{1,0:T(1,128)} %bitcast.4, bf16[1,512,2048]{2,1,0:T(8,128)(2,1)} %ein_h.1, bf16[1,2048,512]{2,1,0:T(8,128)(2,1)} %eout_h.1, bf16[2,16,512]{2,1,0:T(8,128)(2,1)} %sin_h.1, ...), custom_call_target="tpu_custom_call" | custom-call | tf_op jit(solution)/shard_map/exchange/pallas_call | solution.py:434
  64.5 2.0 %mix.1 = bf16[12,256,512]{2,1,0:T(8,128)(2,1)} custom-call(bf16[4,256,512]{2,1,0:T(8,128)(2,1)S(1)} %get-tuple-element.7.rows_r, bf16[12,256,128]{2,1,0:T(8,128)(2,1)S(1)} %get-tuple-element.8.w_r), custom_call_target="tpu_custom_call" | custom-call | tf_op jit(solution)/shard_map/mix/pallas_call | solution.py:486

commit v4 on v3

--- a/solution.py
+++ b/solution.py
@@ -188,7 +188,8 @@
     def along_z(src, slot, k, dz):
         return remote(src, wbuf.at[(d, 0) + slot], zsend, zrecv.at[k], toward(0, dz, 0, 0))
 
-    near = [along_z(wbuf.at[d, 0, 0], (i,), 0, ZSTEP[i]) for i in (1, 2, 3, 4)]
+    near = [along_z(wbuf.at[d, 0, 0], (1,), 0, 1), along_z(wbuf.at[d, 0, 0], (2,), 0, 7)]
+    next_near = [along_z(wbuf.at[d, 0, 1], (3,), 2, 1), along_z(wbuf.at[d, 0, 2], (4,), 2, 7)]
     far = [
         along_z(wbuf.at[d, 0, 3], (5,), 1, 1),
         along_z(wbuf.at[d, 0, 4], (6,), 1, 7),
@@ -234,21 +235,21 @@
     dispatch(0, 2, 4)
     dispatch(1, 0, 2)
     with jax.named_scope("nearwait"):
-        bytes_of(wbuf.at[d, 0, pl.ds(1, 4)], zrecv.at[0]).wait()
+        bytes_of(wbuf.at[d, 0, pl.ds(1, 2)], zrecv.at[0]).wait()
+    for k in next_near:
+        k.start()
+    dispatch(1, 2, 4)
+    dispatch(2, 0, 2)
+    for k in quad:
+        k.start()
+    with jax.named_scope("nextwait"):
+        bytes_of(wbuf.at[d, 0, pl.ds(3, 2)], zrecv.at[2]).wait()
     for k in far:
         k.start()
     for k in along_y[1].values():
         k.start()
     swap[1][0].start()
-    dispatch(1, 2, 4)
-    for k in quad:
-        k.start()
-    with jax.named_scope("farwait"):
-        bytes_of(wbuf.at[d, 0, pl.ds(5, 3)], zrecv.at[1]).wait()
-    for k in along_y[2].values():
-        k.start()
-    swap[2][0].start()
-    dispatch(2)
+    dispatch(2, 2, 4)
     dispatch(3)
     y_arrived(0)
     for k in big:
@@ -311,6 +312,11 @@
             shared_block(p, b, up, down)
 
     serve(0)
+    with jax.named_scope("farwait"):
+        bytes_of(wbuf.at[d, 0, pl.ds(5, 3)], zrecv.at[1]).wait()
+    for k in along_y[2].values():
+        k.start()
+    swap[2][0].start()
     y_arrived(1)
     serve(1)
     with jax.named_scope("quadwait"):
@@ -468,7 +474,7 @@
             dma, dma,
             dma, dma((2,)),
             dma, dma,
-            dma, dma((2,)),
+            dma, dma((3,)),
             dma, dma((3,)),
             dma, dma((2,)),
             dma, dma,

time: 66.5 us -> 65.9 us (level)
  no operation moved by 1% of the time
where the time goes in v4:
time: 65.9 us
  Pallas kernels  65.9 us (100%)
    pallas_call x1, Pallas kernels, on_device(): pl.pallas_call(exchange, out_shape=(jax.ShapeDtypeStruct((4, TOK, D), BF)...  63.9 us
    pallas_call x1, Pallas kernels, on_device(): pl.pallas_call(mix, out_shape=jax.ShapeDtypeStruct((TASKS, TOK, D), BF),...  1.97 us

profile of v4, /device:TPU:1, one launch (start us, length us, event | category | flops | bytes accessed | tf_op | source)
XLA Modules:
  0.0 65.9 jit_solution(12820102764113487670)
XLA Ops:
  0.0 63.9 %exchange.1 = (bf16[4,256,512]{2,1,0:T(8,128)(2,1)S(1)}, bf16[12,256,128]{2,1,0:T(8,128)(2,1)S(1)}) custom-call(bf16[256,512]{1,0:T(8,128)(2,1)} %tok_h.1, s32[2,256]{1,0:T(2,128)} %bitcast.3, s32[1,128]{1,0:T(1,128)} %bitcast.4, bf16[1,512,2048]{2,1,0:T(8,128)(2,1)} %ein_h.1, bf16[1,2048,512]{2,1,0:T(8,128)(2,1)} %eout_h.1, bf16[2,16,512]{2,1,0:T(8,128)(2,1)} %sin_h.1, ...), custom_call_target="tpu_custom_call" | custom-call | tf_op jit(solution)/shard_map/exchange/pallas_call | solution.py:440
  63.9 2.0 %mix.1 = bf16[12,256,512]{2,1,0:T(8,128)(2,1)} custom-call(bf16[4,256,512]{2,1,0:T(8,128)(2,1)S(1)} %get-tuple-element.7.rows_r, bf16[12,256,128]{2,1,0:T(8,128)(2,1)S(1)} %get-tuple-element.8.w_r), custom_call_target="tpu_custom_call" | custom-call | tf_op jit(solution)/shard_map/mix/pallas_call | solution.py:492

commit v5 on v4

--- a/solution.py
+++ b/solution.py
@@ -280,7 +280,14 @@
         if q == SELF // PER:
             back[SELF : SELF + 1] = made[0:1]
         with jax.named_scope("logsend"):
-            each(q, 0, 4, -1, lambda n, to: remote(lret.at[n], lback.at[n], lsend, lrecv, to).start())
+            if q < CH - 1:
+                each(q, 0, 4, -1, lambda n, to: remote(lret.at[n], lback.at[n], lsend, lrecv, to).start())
+            else:
+                for i in (7, 6, 5, 4, 3, 2, 1, 0):
+                    for dy in (2, 1, 3, 0):
+                        n = q * PER + dy * 8 + i
+                        to = toward(1 - q // 2, -ZSTEP[i] % 8, 4 - dy, q % 2)
+                        remote(lret.at[n], lback.at[n], lsend, lrecv, to).start()
         with jax.named_scope("retsend"):
             if q < CH - 1:
                 each(q, 0, 4, -1, lambda n, to: remote(ret.at[n], back.at[n], rsend, rrecv.at[q], to).start())
@@ -322,8 +329,8 @@
     with jax.named_scope("quadwait"):
         bytes_of(tokq.at[pl.ds(1, 2)], trecv.at[0]).wait()
         passed_on.start()
+    serve(2)
     y_arrived(2)
-    serve(2)
     passed_on.wait_recv()
     shared_piece(0)
     serve(3)

time: 65.9 us -> 65.9 us (level)
  no operation moved by 1% of the time
where the time goes in v5:
time: 65.9 us
  Pallas kernels  65.9 us (100%)
    pallas_call x1, Pallas kernels, on_device(): pl.pallas_call(exchange, out_shape=(jax.ShapeDtypeStruct((4, TOK, D), BF)...  63.9 us
    pallas_call x1, Pallas kernels, on_device(): pl.pallas_call(mix, out_shape=jax.ShapeDtypeStruct((TASKS, TOK, D), BF),...  1.97 us

profile of v5, /device:TPU:1, one launch (start us, length us, event | category | flops | bytes accessed | tf_op | source)
XLA Modules:
  0.0 65.9 jit_solution(4763984145801203410)
XLA Ops:
  0.0 63.9 %exchange.1 = (bf16[4,256,512]{2,1,0:T(8,128)(2,1)S(1)}, bf16[12,256,128]{2,1,0:T(8,128)(2,1)S(1)}) custom-call(bf16[256,512]{1,0:T(8,128)(2,1)} %tok_h.1, s32[2,256]{1,0:T(2,128)} %bitcast.3, s32[1,128]{1,0:T(1,128)} %bitcast.4, bf16[1,512,2048]{2,1,0:T(8,128)(2,1)} %ein_h.1, bf16[1,2048,512]{2,1,0:T(8,128)(2,1)} %eout_h.1, bf16[2,16,512]{2,1,0:T(8,128)(2,1)} %sin_h.1, ...), custom_call_target="tpu_custom_call" | custom-call | tf_op jit(solution)/shard_map/exchange/pallas_call | solution.py:447
  63.9 2.0 %mix.1 = bf16[12,256,512]{2,1,0:T(8,128)(2,1)} custom-call(bf16[4,256,512]{2,1,0:T(8,128)(2,1)S(1)} %get-tuple-element.7.rows_r, bf16[12,256,128]{2,1,0:T(8,128)(2,1)S(1)} %get-tuple-element.8.w_r), custom_call_target="tpu_custom_call" | custom-call | tf_op jit(solution)/shard_map/mix/pallas_call | solution.py:499
